TPU v7x, 32 devices: a whole 2x2x4 slice. The times are simulated.
32 devices in a mesh: seq: 8 (over y, x, core), fsdp: 4 (over z).
Axes of the slice: x: 2, y: 2, z: 4, core: 2. Of those that a mesh axis runs over, the one named last changes fastest.
Arguments:
- hidden_in: bfloat16 [4, 1536, 2048], P('fsdp', 'seq'), may hold values from -6 to 6
- weight_query: bfloat16 [2048, 2048], P(('seq', 'fsdp')), may hold values from -0.125 to 0.125
- weight_key: bfloat16 [2048, 2048], P(('seq', 'fsdp')), may hold values from -0.125 to 0.125
- weight_value: bfloat16 [2048, 2048], P(('seq', 'fsdp')), may hold values from -0.125 to 0.125
- weight_output: bfloat16 [2048, 2048], P(('seq', 'fsdp')), may hold values from -2 to 2
- weight_router: bfloat16 [2048, 32], P(('seq', 'fsdp')), may hold values from -0.0625 to 0.0625
- attention_gain: bfloat16 [2048], P(('seq', 'fsdp')), may hold values from 0.5 to 1.5
- mixture_gain: bfloat16 [2048], P(('seq', 'fsdp')), may hold values from 0.5 to 1.5
- queries_gain: bfloat16 [2048], P(('seq', 'fsdp')), may hold values from 0.5 to 1.5
- keys_gain: bfloat16 [2048], P(('seq', 'fsdp')), may hold values from 0.5 to 1.5
- weight_gate: bfloat16 [32, 2048, 1024], P('seq', 'fsdp'), may hold values from -0.125 to 0.125
- weight_up: bfloat16 [32, 2048, 1024], P('seq', 'fsdp'), may hold values from -0.125 to 0.125
- weight_down: bfloat16 [32, 1024, 2048], P('seq', 'fsdp'), may hold values from -0.75 to 0.75
- cotangent: bfloat16 [4, 1536, 2048], P('fsdp', 'seq'), may hold values from -6 to 6
- token_order: int32 [4, 1536], P('fsdp'), may hold values from 0 to 1535, each once within a row
- sequence_lengths: int32 [4, 2], P('fsdp'), may hold values from 1 to 1024, 1536 in all within a row
- expert_choice: int32 [4, 1536, 8], P('fsdp', 'seq'), may hold values from 0 to 31, all different within a row
Outputs:
- block_out: bfloat16 [4, 1536, 2048], P('fsdp', 'seq')
- grad_hidden: bfloat16 [4, 1536, 2048], P('fsdp', 'seq')
- grad_query: float32 [2048, 2048], P(('seq', 'fsdp'))
- grad_key: float32 [2048, 2048], P(('seq', 'fsdp'))
- grad_value: float32 [2048, 2048], P(('seq', 'fsdp'))
- grad_output: float32 [2048, 2048], P(('seq', 'fsdp'))
- grad_router: float32 [2048, 32], P(('seq', 'fsdp'))
- grad_attention_gain: float32 [2048], P(('seq', 'fsdp'))
- grad_mixture_gain: float32 [2048], P(('seq', 'fsdp'))
- grad_queries_gain: float32 [2048], P(('seq', 'fsdp'))
- grad_keys_gain: float32 [2048], P(('seq', 'fsdp'))
- grad_gate: float32 [32, 2048, 1024], P('seq', 'fsdp')
- grad_up: float32 [32, 2048, 1024], P('seq', 'fsdp')
- grad_down: float32 [32, 1024, 2048], P('seq', 'fsdp')
Inputs may be any that keep to these rules, and one draw needn't show every extreme that they name: Each group's row of token_order is a permutation. `sequence_lengths`: each group's lengths sum to 1536; none is longer than 1024. `expert_choice`: a token names 8 different experts; every expert is named by some token.
All inputs are finite; a program needn't handle non-finite values.
Results may differ from a plain program's by a relative error of at most 0.017.
Values may be sent and summed in bfloat16 or wider, within the bound.
A program may use at most 384 MiB of HBM per device.

v0:
```python
import jax
import jax.numpy as jnp
from jax import lax
from jax.sharding import PartitionSpec as P

HEAD_DIM = 128


highest = lax.Precision.HIGHEST
rope_base = 50000.0
norm_eps = 1e-06
masked_score = -1e30


def rms_scale(values, scaling):
    return (
        values * lax.rsqrt(jnp.mean(values * values, axis=-1, keepdims=True) + norm_eps) * scaling
    )


def rotate(values, position):
    half_width = values.shape[-1] // 2
    exponents = jnp.arange(half_width, dtype=jnp.float32) * (2.0 / values.shape[-1])
    frequency = jnp.power(rope_base, -exponents)
    angles = position.astype(jnp.float32)[:, None] * frequency[None, :]
    cosine = jnp.cos(angles)[:, None, :]
    sine_table = jnp.sin(angles)[:, None, :]
    first_half = values[..., :half_width]
    second_half = values[..., half_width:]
    return jnp.concatenate(
        [
            first_half * cosine - second_half * sine_table,
            second_half * cosine + first_half * sine_table,
        ],
        axis=-1,
    )


def layout(places, lengths):
    cumulative = jnp.cumsum(lengths)
    starts = cumulative - lengths
    segment = jnp.sum((places[:, None] >= cumulative[None, :]).astype(jnp.int32), axis=1)
    picked = segment[:, None] == jnp.arange(lengths.shape[0], dtype=jnp.int32)[None, :]
    position = places - jnp.sum(jnp.where(picked, starts[None, :], 0), axis=1)
    return (segment, position)


def gate_softmax(logits, chosen_ids):
    picked = chosen_ids[..., None] == jnp.arange(logits.shape[-1], dtype=jnp.int32)
    chosen = jnp.sum(jnp.where(picked, logits[:, None, :], 0.0), axis=-1)
    peak_score = jnp.max(chosen, axis=-1, keepdims=True)
    weights = jnp.exp(chosen - peak_score)
    return weights / jnp.sum(weights, axis=-1, keepdims=True)


def norm_rotate(raw_values, scaling, position):
    row_count = raw_values.shape[0]
    normed = rms_scale(raw_values, scaling).reshape(row_count, -1, HEAD_DIM)
    return rotate(normed, position).reshape(row_count, -1)


def gather_experts(weight_gate, weight_up, weight_down):
    return (
        lax.all_gather(weight_gate, "fsdp", axis=1, tiled=True),
        lax.all_gather(weight_up, "fsdp", axis=1, tiled=True),
        lax.all_gather(weight_down, "fsdp", axis=1, tiled=True),
    )


def score_block(query_rows, row_segment, head_keys, segment, score_scale):
    scores = (
        jnp.einsum("qhd,khd->hqk", query_rows, head_keys, preferred_element_type=jnp.float32)
        * score_scale
    )
    return jnp.where((row_segment[:, None] == segment[None, :])[None], scores, masked_score)


def body(
    hidden_in,
    weight_query,
    weight_key,
    weight_value,
    weight_output,
    weight_router,
    attention_gain,
    mixture_gain,
    queries_gain,
    keys_gain,
    weight_gate,
    weight_up,
    weight_down,
    cotangent,
    token_order,
    sequence_lengths,
    expert_choice,
):
    seq_count = lax.axis_size("seq")
    seq_place = lax.axis_index("seq")
    inputs = hidden_in[0].astype(jnp.float32)
    tokens = inputs.shape[0]
    group = tokens * seq_count
    width = inputs.shape[1]
    gathered = (
        lax.all_gather(weight_query, ("seq", "fsdp"), axis=0, tiled=True),
        lax.all_gather(weight_key, ("seq", "fsdp"), axis=0, tiled=True),
        lax.all_gather(weight_value, ("seq", "fsdp"), axis=0, tiled=True),
        lax.all_gather(weight_output, ("seq", "fsdp"), axis=0, tiled=True),
        lax.all_gather(weight_router, ("seq", "fsdp"), axis=0, tiled=True),
        lax.all_gather(attention_gain, ("seq", "fsdp"), axis=0, tiled=True),
        lax.all_gather(mixture_gain, ("seq", "fsdp"), axis=0, tiled=True),
        lax.all_gather(queries_gain, ("seq", "fsdp"), axis=0, tiled=True),
        lax.all_gather(keys_gain, ("seq", "fsdp"), axis=0, tiled=True),
    )
    full_query, full_key, full_value, full_output, full_router = (
        gathered[0],
        gathered[1],
        gathered[2],
        gathered[3],
        gathered[4],
    )
    norm_first = gathered[5].astype(jnp.float32)
    norm_second = gathered[6].astype(jnp.float32)
    norm_queries = gathered[7].astype(jnp.float32)
    norm_keys = gathered[8].astype(jnp.float32)
    segment, position = layout(token_order[0], sequence_lengths[0])
    own_position = lax.dynamic_slice_in_dim(position, seq_place * tokens, tokens, 0)
    normed_full, pull_first = jax.vjp(rms_scale, inputs, norm_first)
    normed = normed_full.astype(jnp.bfloat16)
    query_raw = jnp.dot(normed, full_query, preferred_element_type=jnp.float32)
    key_raw = jnp.dot(normed, full_key, preferred_element_type=jnp.float32)
    value_low = jnp.dot(normed, full_value, preferred_element_type=jnp.float32).astype(jnp.bfloat16)
    queries_full, pull_queries = jax.vjp(
        lambda raw_values, scaling: norm_rotate(raw_values, scaling, own_position),
        query_raw,
        norm_queries,
    )
    keys_full, pull_keys = jax.vjp(
        lambda raw_values, scaling: norm_rotate(raw_values, scaling, own_position),
        key_raw,
        norm_keys,
    )
    head_queries, head_keys, head_values = (
        lax.all_to_all(
            queries_full.astype(jnp.bfloat16), "seq", split_axis=1, concat_axis=0, tiled=True
        ),
        lax.all_to_all(
            keys_full.astype(jnp.bfloat16), "seq", split_axis=1, concat_axis=0, tiled=True
        ),
        lax.all_to_all(value_low, "seq", split_axis=1, concat_axis=0, tiled=True),
    )
    head_queries = head_queries.reshape(group, -1, HEAD_DIM)
    head_keys = head_keys.reshape(group, -1, HEAD_DIM)
    head_values = head_values.reshape(group, -1, HEAD_DIM)
    row_block = min(512, group)
    block_count = group // row_block
    score_scale = HEAD_DIM ** (-0.5)

    def forward_block(block_index):
        row_start = block_index * row_block
        query_rows = lax.dynamic_slice_in_dim(head_queries, row_start, row_block, 0)
        row_segment = lax.dynamic_slice_in_dim(segment, row_start, row_block, 0)
        scores = score_block(query_rows, row_segment, head_keys, segment, score_scale)
        peak_score = jnp.max(scores, axis=-1, keepdims=True)
        weights = jnp.exp(scores - peak_score)
        totals = jnp.sum(weights, axis=-1, keepdims=True)
        probabilities = (weights / totals).astype(jnp.bfloat16)
        outcome = jnp.einsum(
            "hqk,khd->qhd", probabilities, head_values, preferred_element_type=jnp.float32
        )
        return (outcome.astype(jnp.bfloat16), (peak_score + jnp.log(totals))[..., 0])

    outcome, log_totals = lax.map(forward_block, jnp.arange(block_count, dtype=jnp.int32))
    attended = lax.all_to_all(
        outcome.reshape(group, -1), "seq", split_axis=0, concat_axis=1, tiled=True
    )
    residual = inputs + jnp.dot(attended, full_output, preferred_element_type=jnp.float32)
    mixed_full, pull_second = jax.vjp(rms_scale, residual, norm_second)
    mixed_low = mixed_full.astype(jnp.bfloat16)
    logits = jnp.dot(mixed_low, full_router, preferred_element_type=jnp.float32)
    chosen_ids = expert_choice[0]
    gate_weights, pull_gates = jax.vjp(
        lambda logit_values: gate_softmax(logit_values, chosen_ids), logits
    )
    experts_all = full_router.shape[1]
    local_experts = weight_gate.shape[0]
    top_count = chosen_ids.shape[1]
    capacity = tokens * top_count // experts_all
    slot_total = experts_all * capacity
    slot_rows = seq_count * capacity
    flat_choice = chosen_ids.reshape(-1)
    onehot = (flat_choice[:, None] == jnp.arange(experts_all, dtype=jnp.int32)[None, :]).astype(
        jnp.int32
    )
    slot_rank = jnp.sum((jnp.cumsum(onehot, axis=0) - onehot) * onehot, axis=1)
    slot_kept = slot_rank < capacity
    target = jnp.where(
        slot_kept,
        flat_choice % local_experts * slot_rows
        + flat_choice // local_experts * capacity
        + slot_rank,
        slot_total,
    )
    slot_owner = (
        jnp.zeros((slot_total,), jnp.int32)
        .at[target]
        .set(jnp.arange(tokens * top_count, dtype=jnp.int32), mode="drop")
    )
    filled = jnp.zeros((slot_total,), jnp.bool_).at[target].set(True, mode="drop")
    zero_low = jnp.zeros((), jnp.bfloat16)
    send_rows = jnp.where(filled[:, None], mixed_low[slot_owner // top_count], zero_low)
    slot_inputs = lax.all_to_all(
        send_rows.reshape(local_experts, seq_count, capacity, width),
        "seq",
        split_axis=1,
        concat_axis=1,
        tiled=True,
    )
    slot_inputs = slot_inputs.reshape(local_experts, slot_rows, width)
    columns = slot_inputs
    gate_sum = jnp.einsum(
        "ecr,erf->ecf",
        columns,
        lax.all_gather(weight_gate, "fsdp", axis=1, tiled=True),
        preferred_element_type=jnp.float32,
    )
    up_sum = jnp.einsum(
        "ecr,erf->ecf",
        columns,
        lax.all_gather(weight_up, "fsdp", axis=1, tiled=True),
        preferred_element_type=jnp.float32,
    )
    hidden_units = (jax.nn.silu(gate_sum) * up_sum).astype(jnp.bfloat16)
    columns = hidden_units
    expert_out = jnp.einsum(
        "ecr,erd->ecd",
        columns,
        lax.all_gather(weight_down, "fsdp", axis=1, tiled=True),
        preferred_element_type=jnp.float32,
    ).astype(jnp.bfloat16)
    returned = lax.all_to_all(
        expert_out.reshape(local_experts, seq_count, capacity, width),
        "seq",
        split_axis=1,
        concat_axis=1,
        tiled=True,
    )
    returned = returned.reshape(slot_total, width)
    safe_slot = jnp.minimum(target, slot_total - 1)
    pair_out = jnp.where(slot_kept[:, None], returned[safe_slot], zero_low).reshape(
        tokens, top_count, width
    )
    block_out = residual + jnp.sum(gate_weights[..., None] * pair_out.astype(jnp.float32), axis=1)
    upstream = cotangent[0].astype(jnp.float32)
    grad_gates = jnp.sum(upstream[:, None, :] * pair_out.astype(jnp.float32), axis=-1)
    grad_pairs = (
        (gate_weights[..., None] * upstream[:, None, :]).astype(jnp.bfloat16).reshape(-1, width)
    )
    grad_send = jnp.where(filled[:, None], grad_pairs[slot_owner], zero_low)
    grad_slots_out = lax.all_to_all(
        grad_send.reshape(local_experts, seq_count, capacity, width),
        "seq",
        split_axis=1,
        concat_axis=1,
        tiled=True,
    )
    grad_slots_out = grad_slots_out.reshape(local_experts, slot_rows, width)
    full_gate, full_up, full_down = gather_experts(weight_gate, weight_up, weight_down)
    grad_units = jnp.einsum(
        "ecd,efd->ecf", grad_slots_out, full_down, preferred_element_type=jnp.float32
    )
    activation_pull = jax.vjp(
        lambda gate_in, up_in: jax.nn.silu(gate_in) * up_in, gate_sum, up_sum
    )[1]
    grad_gate_act, grad_up_act = activation_pull(grad_units)
    grad_gate_low = grad_gate_act.astype(jnp.bfloat16)
    grad_up_low = grad_up_act.astype(jnp.bfloat16)
    grad_slots_in = jnp.einsum(
        "ecf,edf->ecd", grad_gate_low, full_gate, preferred_element_type=jnp.float32
    )
    grad_slots_in = (
        grad_slots_in
        + jnp.einsum("ecf,edf->ecd", grad_up_low, full_up, preferred_element_type=jnp.float32)
    ).astype(jnp.bfloat16)
    gate_term = jnp.einsum(
        "ecd,ecf->edf", slot_inputs, grad_gate_low, preferred_element_type=jnp.float32
    )
    up_term = jnp.einsum(
        "ecd,ecf->edf", slot_inputs, grad_up_low, preferred_element_type=jnp.float32
    )
    down_term = jnp.einsum(
        "ecf,ecd->efd", hidden_units, grad_slots_out, preferred_element_type=jnp.float32
    )
    grad_gate, grad_up, grad_down = (
        lax.psum_scatter(
            gate_term.astype(jnp.bfloat16), "fsdp", scatter_dimension=1, tiled=True
        ).astype(jnp.float32),
        lax.psum_scatter(
            up_term.astype(jnp.bfloat16), "fsdp", scatter_dimension=1, tiled=True
        ).astype(jnp.float32),
        lax.psum_scatter(
            down_term.astype(jnp.bfloat16), "fsdp", scatter_dimension=1, tiled=True
        ).astype(jnp.float32),
    )
    grad_back = lax.all_to_all(
        grad_slots_in.reshape(local_experts, seq_count, capacity, width),
        "seq",
        split_axis=1,
        concat_axis=1,
        tiled=True,
    )
    grad_back = grad_back.reshape(slot_total, width)
    grad_pair_in = jnp.where(slot_kept[:, None], grad_back[safe_slot], zero_low).reshape(
        tokens, top_count, width
    )
    grad_logits = pull_gates(grad_gates)[0]
    router_full = full_router.astype(jnp.float32)
    grad_mixed = jnp.sum(grad_pair_in.astype(jnp.float32), axis=1) + jnp.dot(
        grad_logits, router_full.T, precision=highest
    )
    grad_router = jnp.dot(mixed_low.astype(jnp.float32).T, grad_logits, precision=highest)
    grad_from_second, grad_norm_second = pull_second(grad_mixed)
    grad_residual = upstream + grad_from_second
    grad_branch = grad_residual.astype(jnp.bfloat16)
    grad_output = jnp.einsum("ta,td->ad", attended, grad_branch, preferred_element_type=jnp.float32)
    grad_attended = jnp.einsum(
        "td,ad->ta", grad_branch, full_output, preferred_element_type=jnp.float32
    ).astype(jnp.bfloat16)
    grad_heads = lax.all_to_all(
        grad_attended, "seq", split_axis=1, concat_axis=0, tiled=True
    ).reshape(group, -1, HEAD_DIM)

    def backward_block(running, block_inputs):
        grad_key_sum, grad_value_sum = running
        block_index, log_total = block_inputs
        row_start = block_index * row_block
        query_rows = lax.dynamic_slice_in_dim(head_queries, row_start, row_block, 0)
        row_segment = lax.dynamic_slice_in_dim(segment, row_start, row_block, 0)
        grad_rows = lax.dynamic_slice_in_dim(grad_heads, row_start, row_block, 0)
        scores = score_block(query_rows, row_segment, head_keys, segment, score_scale)
        probabilities = jnp.exp(scores - log_total[..., None])
        grad_probs = jnp.einsum(
            "qhd,khd->hqk", grad_rows, head_values, preferred_element_type=jnp.float32
        )
        inner_sum = jnp.sum(probabilities * grad_probs, axis=-1, keepdims=True)
        grad_scores = (probabilities * (grad_probs - inner_sum)).astype(jnp.bfloat16)
        grad_query_rows = (
            jnp.einsum("hqk,khd->qhd", grad_scores, head_keys, preferred_element_type=jnp.float32)
            * score_scale
        )
        grad_key_sum = (
            grad_key_sum
            + jnp.einsum(
                "hqk,qhd->khd", grad_scores, query_rows, preferred_element_type=jnp.float32
            )
            * score_scale
        )
        grad_value_sum = grad_value_sum + jnp.einsum(
            "hqk,qhd->khd",
            probabilities.astype(jnp.bfloat16),
            grad_rows,
            preferred_element_type=jnp.float32,
        )
        return ((grad_key_sum, grad_value_sum), grad_query_rows)

    zero_heads = jnp.zeros(head_keys.shape, jnp.float32)
    (grad_key_heads, grad_value_heads), grad_query_blocks = lax.scan(
        backward_block,
        (zero_heads, zero_heads),
        (jnp.arange(block_count, dtype=jnp.int32), log_totals),
    )
    grad_query_tok, grad_key_tok, grad_value_tok = (
        lax.all_to_all(
            grad_query_blocks.reshape(group, -1).astype(jnp.bfloat16),
            "seq",
            split_axis=0,
            concat_axis=1,
            tiled=True,
        ),
        lax.all_to_all(
            grad_key_heads.reshape(group, -1).astype(jnp.bfloat16),
            "seq",
            split_axis=0,
            concat_axis=1,
            tiled=True,
        ),
        lax.all_to_all(
            grad_value_heads.reshape(group, -1).astype(jnp.bfloat16),
            "seq",
            split_axis=0,
            concat_axis=1,
            tiled=True,
        ),
    )
    grad_query_raw, grad_norm_queries = pull_queries(grad_query_tok.astype(jnp.float32))
    grad_key_raw, grad_norm_keys = pull_keys(grad_key_tok.astype(jnp.float32))
    grad_query_low = grad_query_raw.astype(jnp.bfloat16)
    grad_key_low = grad_key_raw.astype(jnp.bfloat16)
    grad_normed = jnp.einsum(
        "ta,da->td", grad_query_low, full_query, preferred_element_type=jnp.float32
    )
    grad_normed = grad_normed + jnp.einsum(
        "ta,da->td", grad_key_low, full_key, preferred_element_type=jnp.float32
    )
    grad_normed = grad_normed + jnp.einsum(
        "ta,da->td", grad_value_tok, full_value, preferred_element_type=jnp.float32
    )
    grad_query = jnp.einsum("td,ta->da", normed, grad_query_low, preferred_element_type=jnp.float32)
    grad_key = jnp.einsum("td,ta->da", normed, grad_key_low, preferred_element_type=jnp.float32)
    grad_value = jnp.einsum("td,ta->da", normed, grad_value_tok, preferred_element_type=jnp.float32)
    grad_from_first, grad_norm_first = pull_first(grad_normed)
    grad_hidden = (grad_residual + grad_from_first).astype(jnp.bfloat16)
    dense_grads = (
        lax.psum_scatter(grad_query, ("seq", "fsdp"), scatter_dimension=0, tiled=True),
        lax.psum_scatter(grad_key, ("seq", "fsdp"), scatter_dimension=0, tiled=True),
        lax.psum_scatter(grad_value, ("seq", "fsdp"), scatter_dimension=0, tiled=True),
        lax.psum_scatter(grad_output, ("seq", "fsdp"), scatter_dimension=0, tiled=True),
        lax.psum_scatter(grad_router, ("seq", "fsdp"), scatter_dimension=0, tiled=True),
        lax.psum_scatter(grad_norm_first, ("seq", "fsdp"), scatter_dimension=0, tiled=True),
        lax.psum_scatter(grad_norm_second, ("seq", "fsdp"), scatter_dimension=0, tiled=True),
        lax.psum_scatter(grad_norm_queries, ("seq", "fsdp"), scatter_dimension=0, tiled=True),
        lax.psum_scatter(grad_norm_keys, ("seq", "fsdp"), scatter_dimension=0, tiled=True),
    )
    return (
        block_out.astype(jnp.bfloat16)[None],
        grad_hidden[None],
        dense_grads[0],
        dense_grads[1],
        dense_grads[2],
        dense_grads[3],
        dense_grads[4],
        dense_grads[5],
        dense_grads[6],
        dense_grads[7],
        dense_grads[8],
        grad_gate,
        grad_up,
        grad_down,
    )


def solution(mesh):
    placed = (
        P("fsdp", "seq", None),
        P(("seq", "fsdp"), None),
        P(("seq", "fsdp"), None),
        P(("seq", "fsdp"), None),
        P(("seq", "fsdp"), None),
        P(("seq", "fsdp"), None),
        P(("seq", "fsdp")),
        P(("seq", "fsdp")),
        P(("seq", "fsdp")),
        P(("seq", "fsdp")),
        P("seq", "fsdp", None),
        P("seq", "fsdp", None),
        P("seq", "fsdp", None),
        P("fsdp", "seq", None),
        P("fsdp", None),
        P("fsdp", None),
        P("fsdp", "seq", None),
    )
    return jax.shard_map(
        body,
        mesh=mesh,
        in_specs=placed,
        out_specs=(
            P("fsdp", "seq", None),
            P("fsdp", "seq", None),
            P(("seq", "fsdp"), None),
            P(("seq", "fsdp"), None),
            P(("seq", "fsdp"), None),
            P(("seq", "fsdp"), None),
            P(("seq", "fsdp"), None),
            P(("seq", "fsdp")),
            P(("seq", "fsdp")),
            P(("seq", "fsdp")),
            P(("seq", "fsdp")),
            P("seq", "fsdp", None),
            P("seq", "fsdp", None),
            P("seq", "fsdp", None),
        ),
        check_vma=False,
    )
```

profile of v0, /device:TPU:0, one launch (start us, length us, event | category | flops | bytes accessed | tf_op | source)
XLA Modules:
  0.0 3787.3 jit_solution(9345697627362412261)
XLA Ops:
  12.2 42.9 %all-reduce.13 = (bf16[2048]{0:T(1024)(128)(2,1)S(1)}, bf16[2048]{0:T(1024)(128)(2,1)S(1)}, bf16[2048]{0:T(1024)(128)(2,1)S(1)}, bf16[2048]{0:T(1024)(128)(2,1)S(1)}) all-reduce(bf16[2048]{0:T(1024)(128)(2,1)S(1)} %dynamic-update-slice, bf16[2048]{0:T(1024)(128)(2,1)S(1)} %dynamic-update-slice.1, ...), channel_id=1, replica_groups=mesh['seq'=8,'fsdp'=4] {'seq','fsdp'}, use_global_device_ids=true, to_apply=%add.4 | all-reduce | flops 8192 | bytes 32768
  56.4 34.5 all-gather.9.cloned.1.call-done
  97.9 71.6 %all-gather.11.cloned.1.call-done = bf16[2048,2048]{1,0:T(8,128)(2,1)} async-done(((bf16[64,2048]{1,0:T(8,128)(2,1)}), bf16[2048,2048]{1,0:T(8,128)(2,1)}) %all-gather.11.cloned.1.call-update) | async-done | bytes 8388624 | tf_op jit(solution)/shard_map/all_gather | solution.py:105
  184.3 11.2 all-to-all-done
  200.3 53.4 %all-gather.13.cloned.1.call-done = bf16[2048,2048]{1,0:T(8,128)(2,1)} async-done(((bf16[64,2048]{1,0:T(8,128)(2,1)}), bf16[2048,2048]{1,0:T(8,128)(2,1)}) %all-gather.13.cloned.1.call-update) | async-done | bytes 8388624 | tf_op jit(solution)/shard_map/all_gather | solution.py:106
  264.1 15.9 reduce-window.11
  296.1 28.0 while.27
  332.0 115.1 %all-gather = bf16[32,64,32]{1,2,0:T(8,128)(2,1)S(1)} all-gather(bf16[1,64,32]{1,2,0:T(8,128)(2,1)S(1)} %bitcast.293), channel_id=1, replica_groups=mesh['seq'=8,'fsdp'=4] {'seq','fsdp'}, dimensions={0}, use_global_device_ids=true | all-gather | bytes 135168 | tf_op jit(solution)/shard_map/all_gather | solution.py:108
  449.2 11.2 scatter_custom_fusion
  472.5 7.0 gather_fusion
  483.0 16.3 gather_fusion.2
  499.3 8.2 copy_select_fusion
  507.5 74.8 %all_to_all.133 = bf16[4,8,48,2048]{3,2,0,1:T(8,128)(2,1)} all-to-all(bf16[4,8,48,2048]{3,2,0,1:T(8,128)(2,1)S(1)} %get-tuple-element.337), channel_id=1, replica_groups=mesh['seq'=8,'fsdp'=4] {'seq'}, dimensions={1} | all-to-all | bytes 12582912 | tf_op jit(solution)/shard_map/all_to_all | solution.py:211
  594.0 65.0 %all-to-all-done.6 = bf16[4,8,48,2048]{3,2,0,1:T(8,128)(2,1)} async-done(((bf16[4,8,48,2048]{3,2,0,1:T(8,128)(2,1)}), bf16[4,8,48,2048]{3,2,0,1:T(8,128)(2,1)}, u32[]{:S(2)}, u32[]{:S(2)}) %all-to-all-start.6) | async-done | bytes 6291488 | tf_op jit(solution)/shard_map/all_to_all | solution.py:259
  665.5 15.4 fusion.100
  680.9 231.1 %all-gather.21.cloned.1.call-done = bf16[4,1024,2048]{2,1,0:T(8,128)(2,1)} async-done(((bf16[4,256,2048]{2,1,0:T(8,128)(2,1)}), bf16[4,1024,2048]{2,1,0:T(8,128)(2,1)}) %all-gather.21.cloned.1.call-update) | async-done | bytes 16777232 | tf_op jit(solution)/shard_map/all_gather | solution.py:237
  912.1 13.8 fusion.101
  925.9 272.7 %all-gather.19.cloned.1.call-done = bf16[4,2048,1024]{2,1,0:T(8,128)(2,1)} async-done(((bf16[4,512,1024]{2,1,0:T(8,128)(2,1)}), bf16[4,2048,1024]{2,1,0:T(8,128)(2,1)}) %all-gather.19.cloned.1.call-update) | async-done | bytes 16777232 | tf_op jit(solution)/shard_map/all_gather | solution.py:229
  1198.6 18.4 multiply_convert_fusion.2
  1217.0 13.6 convolution_convert_fusion.3
  1238.8 71.5 %all-to-all-done.5 = bf16[4,8,48,2048]{3,2,0,1:T(8,128)(2,1)} async-done(((bf16[4,8,48,2048]{3,2,0,1:T(8,128)(2,1)}), bf16[4,8,48,2048]{3,2,0,1:T(8,128)(2,1)}, u32[]{:S(2)}, u32[]{:S(2)}) %all-to-all-start.5) | async-done | bytes 6291488 | tf_op jit(solution)/shard_map/all_to_all | solution.py:240
  1316.9 16.3 gather_fusion.1
  1340.6 15.4 convolution_convert_fusion.2
  1356.0 15.2 convolution_convert_fusion.1
  1371.3 15.8 convolution_convert_fusion
  1387.2 14.0 fusion.102
  1401.1 16.0 add_convert_fusion
  1428.7 73.1 %all-to-all-done.7 = bf16[4,8,48,2048]{3,2,0,1:T(8,128)(2,1)} async-done(((bf16[4,8,48,2048]{3,2,0,1:T(8,128)(2,1)}), bf16[4,8,48,2048]{3,2,0,1:T(8,128)(2,1)}, u32[]{:S(2)}, u32[]{:S(2)}) %all-to-all-start.7) | async-done | bytes 6291488 | tf_op jit(solution)/shard_map/all_to_all | solution.py:304
  1508.4 16.8 gather_fusion.3
  1525.3 13.5 convert_reduce_fusion
  1542.3 8.3 fusion.61
  1561.9 12.5 all-to-all-done.8
  1574.6 59.7 %while.28 = (s32[]{:T(128)}, f32[1536,2,128]{0,2,1:T(8,128)}, f32[1536,2,128]{0,2,1:T(8,128)}, bf16[3,512,2,128]{3,1,2,0:T(8,128)(2,1)}, s32[3]{0:T(128)S(1)}, /...) while((s32[]{:T(128)}, f32[1536,2,128]{0,2,1:T(8,128)}, ...), condition=%wide.region_29.30_spmd.clone, body=%wide.region_27.29_spmd.clone.sunk | while | flops 2030304256 | bytes 122454952 | solution.py:366
  1643.6 10.3 all-to-all-done.10
  1659.4 11.4 all-to-all-done.9
  1681.4 8.4 fusion.90
  1694.8 8.3 fusion.92
  1705.8 15.2 all_to_all.134
  1721.2 8.2 fusion.57
  1748.2 40.8 %all-reduce.12 = (f32[2048]{0:T(1024)S(1)}, f32[2048]{0:T(1024)S(1)}, f32[2048]{0:T(1024)S(1)}, f32[2048]{0:T(1024)S(1)}) all-reduce(f32[2048]{0:T(1024)S(1)} %get-tuple-element.258, f32[2048]{0:T(1024)S(1)} %copy-done.53, f32[2048]{0:T(1024)S(1)} %get-tuple-element.254, ...), channel_id=7, replica_groups=mesh['seq'=8,'fsdp'=4] {'seq','fsdp'}, use_global_device_ids=true, to_apply=%region_39.40.clone | all-reduce | flops 8192 | bytes 65536
  1794.2 6.6 convert_element_type.246
  1800.8 237.9 %reduce-scatter.21.cloned.1.call-done = bf16[4,512,1024]{2,1,0:T(8,128)(2,1)} async-done(((bf16[4,2048,1024]{2,1,0:T(8,128)(2,1)}), bf16[4,512,1024]{2,1,0:T(8,128)(2,1)}) %reduce-scatter.21.cloned.1.call-update) | async-done | bytes 4194320 | tf_op jit(solution)/shard_map/reduce_scatter | solution.py:297
  2045.4 276.7 %reduce-scatter.23.cloned.1.call-done = bf16[4,256,2048]{2,1,0:T(8,128)(2,1)} async-done(((bf16[4,1024,2048]{2,1,0:T(8,128)(2,1)}), bf16[4,256,2048]{2,1,0:T(8,128)(2,1)}) %reduce-scatter.23.cloned.1.call-update) | async-done | bytes 4194320 | tf_op jit(solution)/shard_map/reduce_scatter | solution.py:300
  2322.1 6.7 convert_element_type.250
  2328.7 357.3 %reduce-scatter.17.cloned.1.call-done = f32[64,2048]{1,0:T(8,128)} async-done(((f32[2048,2048]{1,0:T(8,128)}), f32[64,2048]{1,0:T(8,128)}) %reduce-scatter.17.cloned.1.call-update) | async-done | bytes 524304 | tf_op jit(solution)/shard_map/reduce_scatter | solution.py:416
  2686.0 364.9 %reduce-scatter.13.cloned.1.call-done = f32[64,2048]{1,0:T(8,128)} async-done(((f32[2048,2048]{1,0:T(8,128)}), f32[64,2048]{1,0:T(8,128)}) %reduce-scatter.13.cloned.1.call-update) | async-done | bytes 524304 | tf_op jit(solution)/shard_map/reduce_scatter | solution.py:414
  3050.9 364.7 %reduce-scatter.11.cloned.1.call-done = f32[64,2048]{1,0:T(8,128)} async-done(((f32[2048,2048]{1,0:T(8,128)}), f32[64,2048]{1,0:T(8,128)}) %reduce-scatter.11.cloned.1.call-update) | async-done | bytes 524304 | tf_op jit(solution)/shard_map/reduce_scatter | solution.py:413
  3415.6 364.7 %reduce-scatter.15.cloned.1.call-done = f32[64,2048]{1,0:T(8,128)} async-done(((f32[2048,2048]{1,0:T(8,128)}), f32[64,2048]{1,0:T(8,128)}) %reduce-scatter.15.cloned.1.call-update) | async-done | bytes 524304 | tf_op jit(solution)/shard_map/reduce_scatter | solution.py:415
  (432 shorter events, 304.7 us)
Async XLA Ops:
  7.2 83.8 %all-gather.9.cloned.1.call-start = ((), (), s32[]{:S(2)}) async-start(), calls=%async_computation.20 | async-start | bytes 8650752 | tf_op jit(solution)/shard_map/all_gather | solution.py:104
  7.9 161.7 %all-gather.11.cloned.1.call-start = ((), (), s32[]{:S(2)}) async-start(), calls=%async_computation.21 | async-start | bytes 8650752 | tf_op jit(solution)/shard_map/all_gather | solution.py:105
  8.7 245.0 %all-gather.13.cloned.1.call-start = ((), (), s32[]{:S(2)}) async-start(), calls=%async_computation.22 | async-start | bytes 8650752 | tf_op jit(solution)/shard_map/all_gather | solution.py:106
  9.4 454.8 %all-gather.15.cloned.1.call-start = ((), (), s32[]{:S(2)}) async-start(), calls=%async_computation.23 | async-start | bytes 8650752 | tf_op jit(solution)/shard_map/all_gather | solution.py:107
  10.0 655.6 %all-gather.17.cloned.1.call-start = ((), (), s32[]{:S(2)}) async-start(), calls=%async_computation.24 | async-start | bytes 20971520 | tf_op jit(solution)/shard_map/all_gather | solution.py:223
  10.6 44.6 %copy-start.64 = (s32[1,1536]{1,0:T(1,128)S(1)}, s32[1,1536]{1,0:T(1,128)}, u32[]{:S(2)}) copy-start(s32[1,1536]{1,0:T(1,128)} %param.35) | copy-start | bytes 18436
  10.6 44.6 %copy-start.75 = (s32[1,2]{1,0:T(1,128)S(1)}, s32[1,2]{1,0:T(1,128)}, u32[]{:S(2)}) copy-start(s32[1,2]{1,0:T(1,128)} %param.36) | copy-start | bytes 28
  10.6 45.1 %copy-start.5 = (bf16[1,192,2048]{2,1,0:T(8,128)(2,1)S(1)}, bf16[1,192,2048]{2,1,0:T(8,128)(2,1)}, u32[]{:S(2)}) copy-start(bf16[1,192,2048]{2,1,0:T(8,128)(2,1)} %param.21) | copy-start | bytes 2359300
  10.6 901.5 %all-gather.21.cloned.1.call-start = ((), (), s32[]{:S(2)}) async-start(), calls=%async_computation.26 | async-start | bytes 20971520 | tf_op jit(solution)/shard_map/all_gather | solution.py:237
  55.1 198.5 %copy-start.40 = (f32[2048]{0:T(1024)}, f32[2048]{0:T(1024)S(1)}, u32[]{:S(2)}) copy-start(f32[2048]{0:T(1024)S(1)} %convert_element_type.200) | copy-start | bytes 24580
  55.1 41.2 %copy-start.42 = (f32[2048]{0:T(1024)}, f32[2048]{0:T(1024)S(1)}, u32[]{:S(2)}) copy-start(f32[2048]{0:T(1024)S(1)} %convert_element_type.202) | copy-start | bytes 24580
  55.2 119.8 %copy-start.44 = (f32[2048]{0:T(1024)}, f32[2048]{0:T(1024)S(1)}, u32[]{:S(2)}) copy-start(f32[2048]{0:T(1024)S(1)} %convert_element_type.205) | copy-start | bytes 24580
  55.9 40.3 %copy-start.61 = (f32[192]{0:T(256)}, f32[192]{0:T(256)S(1)}, u32[]{:S(2)}) copy-start(f32[192]{0:T(256)S(1)} %fusion.43) | copy-start | bytes 2308
  56.0 197.7 %copy-start.48 = (f32[192]{0:T(256)}, f32[192]{0:T(256)S(1)}, u32[]{:S(2)}) copy-start(f32[192]{0:T(256)S(1)} %fusion.84) | copy-start | bytes 2308
  56.4 119.7 %copy-start.33 = (f32[192,64]{1,0:T(8,128)}, f32[192,64]{1,0:T(8,128)S(1)}, u32[]{:S(2)}) copy-start(f32[192,64]{1,0:T(8,128)S(1)} %get-tuple-element.338) | copy-start | bytes 147460
  56.4 119.7 %copy-start.35 = (f32[192,64]{1,0:T(8,128)}, f32[192,64]{1,0:T(8,128)S(1)}, u32[]{:S(2)}) copy-start(f32[192,64]{1,0:T(8,128)S(1)} %get-tuple-element.339) | copy-start | bytes 147460
  179.4 16.1 all-to-all-start
  184.3 15.5 copy-start.52
  195.5 64.3 %all-to-all-start.1 = ((bf16[192,8,256]{2,0,1:T(8,128)(2,1)}), bf16[192,8,256]{2,0,1:T(8,128)(2,1)S(1)}, u32[]{:S(2)}, u32[]{:S(2)}) async-start(bf16[192,8,256]{2,0,1:T(8,128)(2,1)} %copy.183), calls=%async_computation.1 | async-start | bytes 1572864 | tf_op jit(solution)/shard_map/all_to_all | solution.py:146
  199.1 999.6 %all-gather.19.cloned.1.call-start = ((), (), s32[]{:S(2)}) async-start(), calls=%async_computation.25 | async-start | bytes 20971520 | tf_op jit(solution)/shard_map/all_gather | solution.py:229
  259.8 34.0 all-to-all-start.2
  324.1 138.9 %copy-start.2 = (bf16[1536,2,128]{2,0,1:T(8,128)(2,1)}, bf16[1536,2,128]{2,0,1:T(8,128)(2,1)S(1)}, u32[]{:S(2)}) copy-start(bf16[1536,2,128]{2,0,1:T(8,128)(2,1)S(1)} %get-tuple-element.572) | copy-start | bytes 2359300
  324.1 138.9 %copy-start.7 = (bf16[1536,2,128]{2,0,1:T(8,128)(2,1)}, bf16[1536,2,128]{2,0,1:T(8,128)(2,1)S(1)}, u32[]{:S(2)}) copy-start(bf16[1536,2,128]{2,0,1:T(8,128)(2,1)S(1)} %get-tuple-element.597) | copy-start | bytes 2359300
  324.1 138.9 %copy-start.8 = (bf16[1536,2,128]{2,0,1:T(8,128)(2,1)}, bf16[1536,2,128]{2,0,1:T(8,128)(2,1)S(1)}, u32[]{:S(2)}) copy-start(bf16[1536,2,128]{2,0,1:T(8,128)(2,1)S(1)} %get-tuple-element.598) | copy-start | bytes 2359300
  324.1 138.9 %copy-start.29 = (s32[1536]{0:T(1024)}, s32[1536]{0:T(1024)S(1)}, u32[]{:S(2)}) copy-start(s32[1536]{0:T(1024)S(1)} %get-tuple-element.648) | copy-start | bytes 18436
  327.7 135.3 %all-to-all-start.3 = ((bf16[8,192,256]{2,1,0:T(8,128)(2,1)}), bf16[8,192,256]{2,1,0:T(8,128)(2,1)}, u32[]{:S(2)}, u32[]{:S(2)}) async-start(bf16[8,192,256]{2,1,0:T(8,128)(2,1)} %all_to_all.105), calls=%async_computation.3 | async-start | bytes 1572864 | tf_op jit(solution)/shard_map/all_to_all | solution.py:173
  332.0 137.9 %copy-start.46 = (f32[2048]{0:T(1024)}, f32[2048]{0:T(1024)S(1)}, u32[]{:S(2)}) copy-start(f32[2048]{0:T(1024)S(1)} %convert_element_type.208) | copy-start | bytes 24580
  449.1 22.1 copy-start.31
  582.4 76.5 %all-to-all-start.6 = ((bf16[4,8,48,2048]{3,2,0,1:T(8,128)(2,1)}), bf16[4,8,48,2048]{3,2,0,1:T(8,128)(2,1)}, u32[]{:S(2)}, u32[]{:S(2)}) async-start(bf16[4,8,48,2048]{3,2,0,1:T(8,128)(2,1)} %get-tuple-element.336), calls=%async_computation.6 | async-start | bytes 12582912 | tf_op jit(solution)/shard_map/all_to_all | solution.py:259
  1233.8 76.5 %all-to-all-start.5 = ((bf16[4,8,48,2048]{3,2,0,1:T(8,128)(2,1)}), bf16[4,8,48,2048]{3,2,0,1:T(8,128)(2,1)}, u32[]{:S(2)}, u32[]{:S(2)}) async-start(bf16[4,8,48,2048]{3,2,0,1:T(8,128)(2,1)} %copy.200), calls=%async_computation.5 | async-start | bytes 12582912 | tf_op jit(solution)/shard_map/all_to_all | solution.py:240
  1238.7 490.7 %reduce-scatter.25.cloned.1.call-start = ((), (), s32[]{:S(2)}) async-start(), calls=%async_computation.34 | async-start | bytes 1081344
  1340.5 453.6 %reduce-scatter.19.cloned.1.call-start = ((), (), s32[]{:S(2)}) async-start(), calls=%async_computation.31 | async-start | bytes 20971520 | tf_op jit(solution)/shard_map/reduce_scatter | solution.py:294
  1356.0 682.7 %reduce-scatter.21.cloned.1.call-start = ((), (), s32[]{:S(2)}) async-start(), calls=%async_computation.32 | async-start | bytes 20971520 | tf_op jit(solution)/shard_map/reduce_scatter | solution.py:297
  1371.2 950.8 %reduce-scatter.23.cloned.1.call-start = ((), (), s32[]{:S(2)}) async-start(), calls=%async_computation.33 | async-start | bytes 20971520 | tf_op jit(solution)/shard_map/reduce_scatter | solution.py:300
  1423.8 78.0 %all-to-all-start.7 = ((bf16[4,8,48,2048]{3,2,0,1:T(8,128)(2,1)}), bf16[4,8,48,2048]{3,2,0,1:T(8,128)(2,1)}, u32[]{:S(2)}, u32[]{:S(2)}) async-start(bf16[4,8,48,2048]{3,2,0,1:T(8,128)(2,1)} %copy.205), calls=%async_computation.7 | async-start | bytes 12582912 | tf_op jit(solution)/shard_map/all_to_all | solution.py:304
  1428.5 1257.5 %reduce-scatter.17.cloned.1.call-start = ((), (), s32[]{:S(2)}) async-start(), calls=%async_computation.30 | async-start | bytes 17301504 | tf_op jit(solution)/shard_map/reduce_scatter | solution.py:416
  1508.4 16.8 copy-start.38
  1557.2 17.4 copy-start.3
  1557.2 17.4 copy-start.9
  1557.2 17.4 copy-start.30
  1558.2 16.2 all-to-all-start.8
  1637.9 16.1 all-to-all-start.10
  1653.9 16.8 all-to-all-start.9
  1658.1 1392.8 %reduce-scatter.13.cloned.1.call-start = ((), (), s32[]{:S(2)}) async-start(), calls=%async_computation.28 | async-start | bytes 17301504 | tf_op jit(solution)/shard_map/reduce_scatter | solution.py:414
  1689.8 1725.7 %reduce-scatter.11.cloned.1.call-start = ((), (), s32[]{:S(2)}) async-start(), calls=%async_computation.27 | async-start | bytes 17301504 | tf_op jit(solution)/shard_map/reduce_scatter | solution.py:413
  1703.1 2077.1 %reduce-scatter.15.cloned.1.call-start = ((), (), s32[]{:S(2)}) async-start(), calls=%async_computation.29 | async-start | bytes 17301504 | tf_op jit(solution)/shard_map/reduce_scatter | solution.py:415
  1743.9 47.5 %copy-start.62 = (f32[192]{0:T(256)S(1)}, f32[192]{0:T(256)}, u32[]{:S(2)}) copy-start(f32[192]{0:T(256)} %copy-done.61) | copy-start | bytes 2308
  1743.9 47.5 %copy-start.12 = (f32[192,2048]{1,0:T(8,128)S(1)}, f32[192,2048]{1,0:T(8,128)}, u32[]{:S(2)}) copy-start(f32[192,2048]{1,0:T(8,128)} %copy-done.11) | copy-start | bytes 4718596
  (67 other events, 273.8 us)
Sparse Core Ops, SparseCore 0:
  10.9 79.9 all-gather.8
  93.9 75.6 all-gather.10
  172.5 81.0 all-gather.12
  256.4 78.4 all-gather.14
  336.3 289.2 all-gather.16
  627.0 285.0 all-gather.20
  913.7 284.9 all-gather.18
  1340.7 134.6 reduce-scatter.24
  1477.7 276.9 reduce-scatter.18
  1756.9 281.8 reduce-scatter.20
  2041.1 280.9 reduce-scatter.22
  2324.8 361.2 reduce-scatter.16
  2688.9 361.9 reduce-scatter.12
  3053.6 361.9 reduce-scatter.10
  3418.3 361.9 reduce-scatter.14
where the time goes:
time: 3800 us; the launch traced here: 3790 us
  waiting for transfers between devices  2890 us (76%)
  blocking collectives  289 us (8%)
  matrix products  273 us (7%)
  local copies, waits for them, and re-layouts  171 us (4%)
  other arithmetic  104 us (3%)
  starting transfers between devices  42.1 us (1%)
    reduce_scatter x1, waiting for transfers between devices, body(): lax.psum_scatter(grad_key, ('seq', 'fsdp'), scatter_dimension=0, tiled=True)  365 us
    reduce_scatter x1, waiting for transfers between devices, body(): lax.psum_scatter(grad_query, ('seq', 'fsdp'), scatter_dimension=0, tiled=...  365 us
    reduce_scatter x1, waiting for transfers between devices, body(): lax.psum_scatter(grad_value, ('seq', 'fsdp'), scatter_dimension=0, tiled=...  365 us
    reduce_scatter x1, waiting for transfers between devices, body(): lax.psum_scatter(grad_output, ('seq', 'fsdp'), scatter_dimension=0, tiled...  357 us
    reduce_scatter x1, waiting for transfers between devices, body(): lax.psum_scatter(down_term.astype(jnp.bfloat16), 'fsdp', scatter_dimensio...  277 us
    all_gather x1, waiting for transfers between devices, body(): lax.all_gather(weight_up, 'fsdp', axis=1, tiled=True)  273 us
    reduce_scatter x1, waiting for transfers between devices, body(): lax.psum_scatter(up_term.astype(jnp.bfloat16), 'fsdp', scatter_dimension=...  238 us
    all_gather x1, waiting for transfers between devices, body(): lax.all_gather(weight_down, 'fsdp', axis=1, tiled=True)  231 us
  transfers between devices with their start and end apart: 25, of which 18 were waited for; matrix products, arithmetic and copies ran while one was open for 12% of the time, Pallas kernels for 0%

commit v1 on v0

v1 whole, which is shorter than its diff:
```python
import jax
import jax.numpy as jnp
from jax import lax
from jax.sharding import PartitionSpec as P

HEAD_DIM = 128


highest = lax.Precision.HIGHEST
rope_base = 50000.0
norm_eps = 1e-06
masked_score = -1e30


def rms_scale(values, scaling):
    return (
        values * lax.rsqrt(jnp.mean(values * values, axis=-1, keepdims=True) + norm_eps) * scaling
    )


def rotate(values, position):
    half_width = values.shape[-1] // 2
    exponents = jnp.arange(half_width, dtype=jnp.float32) * (2.0 / values.shape[-1])
    frequency = jnp.power(rope_base, -exponents)
    angles = position.astype(jnp.float32)[:, None] * frequency[None, :]
    cosine = jnp.cos(angles)[:, None, :]
    sine_table = jnp.sin(angles)[:, None, :]
    first_half = values[..., :half_width]
    second_half = values[..., half_width:]
    return jnp.concatenate(
        [
            first_half * cosine - second_half * sine_table,
            second_half * cosine + first_half * sine_table,
        ],
        axis=-1,
    )


def layout(places, lengths):
    cumulative = jnp.cumsum(lengths)
    starts = cumulative - lengths
    segment = jnp.sum((places[:, None] >= cumulative[None, :]).astype(jnp.int32), axis=1)
    picked = segment[:, None] == jnp.arange(lengths.shape[0], dtype=jnp.int32)[None, :]
    position = places - jnp.sum(jnp.where(picked, starts[None, :], 0), axis=1)
    return (segment, position)


def gate_softmax(logits, chosen_ids):
    picked = chosen_ids[..., None] == jnp.arange(logits.shape[-1], dtype=jnp.int32)
    chosen = jnp.sum(jnp.where(picked, logits[:, None, :], 0.0), axis=-1)
    peak_score = jnp.max(chosen, axis=-1, keepdims=True)
    weights = jnp.exp(chosen - peak_score)
    return weights / jnp.sum(weights, axis=-1, keepdims=True)


def norm_rotate(raw_values, scaling, position):
    row_count = raw_values.shape[0]
    normed = rms_scale(raw_values, scaling).reshape(row_count, -1, HEAD_DIM)
    return rotate(normed, position).reshape(row_count, -1)


def score_block(query_rows, row_segment, head_keys, segment, score_scale):
    scores = (
        jnp.einsum("qhd,khd->hqk", query_rows, head_keys, preferred_element_type=jnp.float32)
        * score_scale
    )
    return jnp.where((row_segment[:, None] == segment[None, :])[None], scores, masked_score)


AXES = ("seq", "fsdp")
low_type = jnp.bfloat16


def rotate_back(values, position):
    half_width = values.shape[-1] // 2
    exponents = jnp.arange(half_width, dtype=jnp.float32) * (2.0 / values.shape[-1])
    frequency = jnp.power(rope_base, -exponents)
    angles = position.astype(jnp.float32)[:, None] * frequency[None, :]
    cosine = jnp.cos(angles)[:, None, :]
    sine_table = jnp.sin(angles)[:, None, :]
    first_half = values[..., :half_width]
    second_half = values[..., half_width:]
    return jnp.concatenate(
        [
            first_half * cosine + second_half * sine_table,
            second_half * cosine - first_half * sine_table,
        ],
        axis=-1,
    )


def swap(values, axis_name, dim):
    return lax.all_to_all(values, axis_name, split_axis=dim, concat_axis=dim, tiled=True)


def dot32(spec, left, right):
    return jnp.einsum(spec, left, right, preferred_element_type=jnp.float32)


def attention_forward(head_queries, head_keys, head_values, segment, score_scale):
    group = head_queries.shape[0]
    row_block = min(512, group)
    block_count = group // row_block

    def forward_block(block_index):
        row_start = block_index * row_block
        query_rows = lax.dynamic_slice_in_dim(head_queries, row_start, row_block, 0)
        row_segment = lax.dynamic_slice_in_dim(segment, row_start, row_block, 0)
        scores = score_block(query_rows, row_segment, head_keys, segment, score_scale)
        peak_score = jnp.max(scores, axis=-1, keepdims=True)
        weights = jnp.exp(scores - peak_score)
        totals = jnp.sum(weights, axis=-1, keepdims=True)
        probabilities = (weights / totals).astype(low_type)
        outcome = dot32("hqk,khd->qhd", probabilities, head_values)
        return (outcome.astype(low_type), (peak_score + jnp.log(totals))[..., 0])

    outcome, log_totals = lax.map(forward_block, jnp.arange(block_count, dtype=jnp.int32))
    return outcome.reshape(group, -1), log_totals


def attention_backward(head_queries, head_keys, head_values, grad_heads, segment, log_totals, score_scale):
    group = head_queries.shape[0]
    row_block = min(512, group)
    block_count = group // row_block

    def backward_block(running, block_inputs):
        grad_key_sum, grad_value_sum = running
        block_index, log_total = block_inputs
        row_start = block_index * row_block
        query_rows = lax.dynamic_slice_in_dim(head_queries, row_start, row_block, 0)
        row_segment = lax.dynamic_slice_in_dim(segment, row_start, row_block, 0)
        grad_rows = lax.dynamic_slice_in_dim(grad_heads, row_start, row_block, 0)
        scores = score_block(query_rows, row_segment, head_keys, segment, score_scale)
        probabilities = jnp.exp(scores - log_total[..., None])
        grad_probs = dot32("qhd,khd->hqk", grad_rows, head_values)
        inner_sum = jnp.sum(probabilities * grad_probs, axis=-1, keepdims=True)
        grad_scores = (probabilities * (grad_probs - inner_sum)).astype(low_type)
        grad_query_rows = dot32("hqk,khd->qhd", grad_scores, head_keys) * score_scale
        grad_key_sum = grad_key_sum + dot32("hqk,qhd->khd", grad_scores, query_rows) * score_scale
        grad_value_sum = grad_value_sum + dot32(
            "hqk,qhd->khd", probabilities.astype(low_type), grad_rows
        )
        return ((grad_key_sum, grad_value_sum), grad_query_rows)

    zero_heads = jnp.zeros(head_keys.shape, jnp.float32)
    (grad_keys, grad_values), grad_queries = lax.scan(
        backward_block,
        (zero_heads, zero_heads),
        (jnp.arange(block_count, dtype=jnp.int32), log_totals),
    )
    return grad_queries.reshape(head_queries.shape), grad_keys, grad_values


def body(
    hidden_in,
    weight_query,
    weight_key,
    weight_value,
    weight_output,
    weight_router,
    attention_gain,
    mixture_gain,
    queries_gain,
    keys_gain,
    weight_gate,
    weight_up,
    weight_down,
    cotangent,
    token_order,
    sequence_lengths,
    expert_choice,
):
    seq_count = lax.axis_size("seq")
    seq_place = lax.axis_index("seq")
    fsdp_count = lax.axis_size("fsdp")
    fsdp_place = lax.axis_index("fsdp")
    inputs_low = hidden_in[0]
    tokens, width = inputs_low.shape
    group = tokens * seq_count
    shard_rows, columns_all = weight_query.shape
    columns = columns_all // seq_count
    local_heads = columns // HEAD_DIM
    score_scale = HEAD_DIM ** (-0.5)
    chosen_ids = expert_choice[0]
    top_count = chosen_ids.shape[1]

    small = jnp.concatenate(
        [
            weight_router,
            attention_gain[:, None],
            mixture_gain[:, None],
            queries_gain[:, None],
            keys_gain[:, None],
        ],
        axis=1,
    )
    small = lax.all_gather(small, AXES, axis=0, tiled=True)
    experts_all = weight_router.shape[1]
    full_router = small[:, :experts_all]
    norm_first = small[:, experts_all].astype(jnp.float32)
    norm_second = small[:, experts_all + 1].astype(jnp.float32)
    own_columns = lax.dynamic_slice_in_dim(
        small[:, experts_all + 2 :].astype(jnp.float32), seq_place * columns, columns, 0
    )
    norm_queries, norm_keys = own_columns[:, 0], own_columns[:, 1]

    inputs_group = lax.all_gather(inputs_low, "seq", axis=0, tiled=True).astype(jnp.float32)
    qkv_parts = jnp.stack(
        [w.reshape(shard_rows, seq_count, columns) for w in (weight_query, weight_key, weight_value)]
    )
    qkv_parts = swap(qkv_parts.transpose(2, 0, 1, 3), "seq", 0)
    qkv_parts = lax.all_gather(qkv_parts, "fsdp", axis=0, tiled=False)
    weight_qkv = qkv_parts.transpose(1, 0, 3, 2, 4).reshape(width, 3 * columns)
    full_output = lax.all_gather(weight_output, AXES, axis=0, tiled=True)

    local_experts, row_share, hidden_count = weight_gate.shape
    parts = fsdp_count // local_experts
    assert parts * local_experts == fsdp_count
    strip = hidden_count // (fsdp_count * parts)

    def to_owner(weights):
        pieces = weights.reshape(local_experts, row_share, fsdp_count, parts, strip)
        pieces = pieces.transpose(0, 3, 1, 2, 4)
        pieces = pieces.reshape(fsdp_count, row_share, fsdp_count * strip)
        return swap(pieces, "fsdp", 0).reshape(width, fsdp_count * strip)

    def from_owner(grads):
        pieces = grads.reshape(fsdp_count, row_share, fsdp_count * strip)
        pieces = swap(pieces, "fsdp", 0)
        pieces = pieces.reshape(local_experts, parts, row_share, fsdp_count, strip)
        pieces = pieces.transpose(0, 2, 3, 1, 4)
        return pieces.reshape(local_experts, row_share, hidden_count).astype(jnp.float32)

    own_down = swap(weight_down.reshape(fsdp_count, strip, width), "fsdp", 0).reshape(-1, width)
    own_gate = to_owner(weight_gate)
    own_up = to_owner(weight_up)

    capacity = tokens * top_count // experts_all
    lanes = seq_count * capacity
    lane = jnp.arange(lanes, dtype=jnp.int32)
    lane_expert = lane // capacity * local_experts + fsdp_place // parts
    lane_slot = (lane % capacity).astype(jnp.float32)
    choice_all = lax.all_gather(chosen_ids, "fsdp", axis=0, tiled=False)
    named = jnp.any(choice_all[..., None] == lane_expert, axis=2)
    earlier = (
        jnp.arange(tokens, dtype=jnp.int32)[:, None] > jnp.arange(tokens, dtype=jnp.int32)[None, :]
    ).astype(low_type)
    rank = dot32("tu,guj->gtj", earlier, named.astype(low_type))
    holds = named & (rank == lane_slot)
    place = holds.astype(low_type)

    def to_slots(rows):
        sent = jnp.einsum("gtj,gtd->gjd", place, rows)
        sent = sent.reshape(fsdp_count, seq_count, capacity, width)
        return swap(sent, "seq", 1).reshape(fsdp_count * lanes, width)

    def from_slots(rows, matrix):
        back = swap(rows.reshape(fsdp_count, seq_count, capacity, width), "seq", 1)
        mixed = dot32("gtj,gjd->gtd", matrix, back.reshape(fsdp_count, lanes, width))
        parts_back = swap(mixed.astype(low_type), "fsdp", 0)
        return jnp.sum(parts_back.astype(jnp.float32), axis=0)

    cotangent_low = cotangent[0]
    cotangent_all = lax.all_gather(cotangent_low, "fsdp", axis=0, tiled=False)
    slot_cotangent = to_slots(cotangent_all)
    units_cotangent = dot32("cd,fd->cf", slot_cotangent, own_down)

    segment, position = layout(token_order[0], sequence_lengths[0])
    first_scale = lax.rsqrt(jnp.mean(inputs_group * inputs_group, axis=-1, keepdims=True) + norm_eps)
    normed = (inputs_group * first_scale * norm_first).astype(low_type)
    raw = dot32("td,dc->tc", normed, weight_qkv)
    query_raw, key_raw = raw[:, :columns], raw[:, columns : 2 * columns]
    head_values = raw[:, 2 * columns :].astype(low_type).reshape(group, local_heads, HEAD_DIM)

    def group_means(left, right):
        sums = jnp.stack([jnp.sum(left, axis=-1), jnp.sum(right, axis=-1)])
        sums = jnp.sum(lax.all_gather(sums, "seq", axis=0, tiled=False), axis=0)
        return (sums / columns_all)[..., None]

    squares = group_means(query_raw * query_raw, key_raw * key_raw)
    query_scale, key_scale = lax.rsqrt(squares[0] + norm_eps), lax.rsqrt(squares[1] + norm_eps)
    query_unit, key_unit = query_raw * query_scale, key_raw * key_scale

    def spin(values, scaling):
        return rotate((values * scaling).reshape(group, -1, HEAD_DIM), position).astype(low_type)

    head_queries, head_keys = spin(query_unit, norm_queries), spin(key_unit, norm_keys)
    attended_heads, log_totals = attention_forward(
        head_queries, head_keys, head_values, segment, score_scale
    )
    attended = lax.all_to_all(attended_heads, "seq", split_axis=0, concat_axis=1, tiled=True)
    inputs = inputs_low.astype(jnp.float32)
    residual = inputs + dot32("ta,ad->td", attended, full_output)

    second_scale = lax.rsqrt(jnp.mean(residual * residual, axis=-1, keepdims=True) + norm_eps)
    second_unit = residual * second_scale
    mixed_low = (second_unit * norm_second).astype(low_type)
    mixed_all = lax.all_gather(mixed_low, "fsdp", axis=0, tiled=False)
    logits = dot32("td,de->te", mixed_low, full_router)
    gate_weights = gate_softmax(logits, chosen_ids)
    gates_all = lax.all_gather(gate_weights, "fsdp", axis=0, tiled=False)
    lane_gate = jnp.sum(
        jnp.where(choice_all[..., None] == lane_expert, gates_all[..., None], 0.0), axis=2
    )
    place_gate = jnp.where(holds, lane_gate, 0.0)
    slot_gate = jnp.sum(place_gate, axis=1).reshape(fsdp_count, seq_count, capacity)
    slot_gate = swap(slot_gate, "seq", 1).reshape(-1, 1)

    slot_inputs = to_slots(mixed_all)
    gate_act = dot32("cd,df->cf", slot_inputs, own_gate)
    up_act = dot32("cd,df->cf", slot_inputs, own_up)
    sigma = jax.nn.sigmoid(gate_act)
    silu = gate_act * sigma
    hidden_units = (silu * up_act).astype(low_type)

    grad_units = slot_gate * units_cotangent
    grad_gate_low = (grad_units * up_act * sigma * (1.0 + gate_act * (1.0 - sigma))).astype(low_type)
    grad_up_low = (grad_units * silu).astype(low_type)
    grad_slots_in = dot32("cf,df->cd", grad_gate_low, own_gate)
    grad_slots_in = (grad_slots_in + dot32("cf,df->cd", grad_up_low, own_up)).astype(low_type)
    from_pairs = from_slots(grad_slots_in, place)

    slot_grad_gate = jnp.sum(hidden_units.astype(jnp.float32) * units_cotangent, axis=-1)
    slot_grad_gate = swap(slot_grad_gate.reshape(fsdp_count, seq_count, capacity), "seq", 1)
    lane_grad = jnp.where(holds, slot_grad_gate.reshape(fsdp_count, 1, lanes), 0.0)
    grad_gates = jnp.sum(
        jnp.where(choice_all[..., None] == lane_expert, lane_grad[:, :, None, :], 0.0), axis=-1
    )
    grad_gates = jnp.sum(swap(grad_gates, "fsdp", 0), axis=0)
    pair_logits = gate_weights * (
        grad_gates - jnp.sum(gate_weights * grad_gates, axis=-1, keepdims=True)
    )
    picked = chosen_ids[..., None] == jnp.arange(experts_all, dtype=jnp.int32)
    grad_logits = jnp.sum(jnp.where(picked, pair_logits[..., None], 0.0), axis=1)

    grad_mixed = from_pairs + jnp.dot(
        grad_logits, full_router.astype(jnp.float32).T, precision=highest
    )
    grad_router = jnp.dot(mixed_low.astype(jnp.float32).T, grad_logits, precision=highest)
    upstream = cotangent_low.astype(jnp.float32)
    scaled = norm_second * grad_mixed
    grad_residual = upstream + second_scale * (
        scaled - second_unit * jnp.mean(second_unit * scaled, axis=-1, keepdims=True)
    )
    grad_mixture_gain = jnp.sum(grad_mixed * second_unit, axis=0)
    grad_branch = grad_residual.astype(low_type)

    grad_attended = dot32("td,ad->ta", grad_branch, full_output).astype(low_type)
    grad_heads = lax.all_to_all(
        grad_attended, "seq", split_axis=1, concat_axis=0, tiled=True
    ).reshape(group, local_heads, HEAD_DIM)
    grad_branch_group = lax.all_gather(grad_branch, "seq", axis=0, tiled=True)

    grad_gate = from_owner(dot32("cd,cf->df", slot_inputs, grad_gate_low).astype(low_type))
    grad_up = from_owner(dot32("cd,cf->df", slot_inputs, grad_up_low).astype(low_type))
    gated_units = (slot_gate * hidden_units.astype(jnp.float32)).astype(low_type)
    down_term = dot32("cf,cd->fd", gated_units, slot_cotangent).astype(low_type)
    grad_down = swap(down_term.reshape(fsdp_count, strip, width), "fsdp", 0)
    grad_down = grad_down.reshape(local_experts, parts * strip, width).astype(jnp.float32)

    expert_out = dot32("cf,fd->cd", hidden_units, own_down).astype(low_type)
    block_out = residual + from_slots(expert_out, place_gate.astype(low_type))

    grad_queries, grad_keys, grad_values = attention_backward(
        head_queries, head_keys, head_values, grad_heads, segment, log_totals, score_scale
    )

    query_back = rotate_back(grad_queries, position).reshape(group, columns)
    key_back = rotate_back(grad_keys, position).reshape(group, columns)
    grad_norms = jnp.concatenate(
        [jnp.sum(query_back * query_unit, axis=0), jnp.sum(key_back * key_unit, axis=0)]
    ).reshape(2, columns)
    query_back, key_back = query_back * norm_queries, key_back * norm_keys
    inner = group_means(query_back * query_unit, key_back * key_unit)
    grad_raw = jnp.concatenate(
        [
            (query_scale * (query_back - query_unit * inner[0])).astype(low_type),
            (key_scale * (key_back - key_unit * inner[1])).astype(low_type),
            grad_values.reshape(group, columns).astype(low_type),
        ],
        axis=1,
    )
    normed_part = dot32("tc,dc->td", grad_raw, weight_qkv).astype(low_type)
    normed_parts = swap(normed_part.reshape(seq_count, tokens, width), "seq", 0)
    grad_normed = jnp.sum(normed_parts.astype(jnp.float32), axis=0)
    own_scale = lax.rsqrt(jnp.mean(inputs * inputs, axis=-1, keepdims=True) + norm_eps)
    first_unit = inputs * own_scale
    grad_attention_gain = jnp.sum(grad_normed * first_unit, axis=0)
    scaled = norm_first * grad_normed
    grad_hidden = (
        grad_residual
        + own_scale * (scaled - first_unit * jnp.mean(first_unit * scaled, axis=-1, keepdims=True))
    ).astype(low_type)

    grad_output = dot32("ta,td->ad", attended_heads, grad_branch_group).astype(low_type)
    grad_output = swap(grad_output.reshape(fsdp_count, shard_rows, width), "fsdp", 0)
    grad_output = jnp.sum(grad_output.astype(jnp.float32), axis=0)
    grad_qkv = dot32("td,tc->dc", normed, grad_raw).astype(low_type)
    grad_qkv = grad_qkv.reshape(seq_count, fsdp_count, shard_rows, 3 * columns)
    grad_qkv = jnp.sum(swap(grad_qkv, "fsdp", 1).astype(jnp.float32), axis=1).astype(low_type)
    grad_qkv = swap(grad_qkv, "seq", 0).reshape(seq_count, shard_rows, 3, columns)
    grad_qkv = grad_qkv.transpose(2, 1, 0, 3).reshape(3, shard_rows, columns_all)
    grad_qkv = grad_qkv.astype(jnp.float32)

    grad_norms = lax.psum_scatter(grad_norms, "fsdp", scatter_dimension=1, tiled=True)
    rows_sum = jnp.concatenate(
        [grad_router, grad_attention_gain[:, None], grad_mixture_gain[:, None]], axis=1
    )
    rows_sum = lax.psum_scatter(rows_sum, AXES, scatter_dimension=0, tiled=True)
    return (
        block_out.astype(low_type)[None],
        grad_hidden[None],
        grad_qkv[0],
        grad_qkv[1],
        grad_qkv[2],
        grad_output,
        rows_sum[:, :experts_all],
        rows_sum[:, experts_all],
        rows_sum[:, experts_all + 1],
        grad_norms[0],
        grad_norms[1],
        grad_gate,
        grad_up,
        grad_down,
    )


def solution(mesh):
    placed = (
        P("fsdp", "seq", None),
        P(("seq", "fsdp"), None),
        P(("seq", "fsdp"), None),
        P(("seq", "fsdp"), None),
        P(("seq", "fsdp"), None),
        P(("seq", "fsdp"), None),
        P(("seq", "fsdp")),
        P(("seq", "fsdp")),
        P(("seq", "fsdp")),
        P(("seq", "fsdp")),
        P("seq", "fsdp", None),
        P("seq", "fsdp", None),
        P("seq", "fsdp", None),
        P("fsdp", "seq", None),
        P("fsdp", None),
        P("fsdp", None),
        P("fsdp", "seq", None),
    )
    return jax.shard_map(
        body,
        mesh=mesh,
        in_specs=placed,
        out_specs=(
            P("fsdp", "seq", None),
            P("fsdp", "seq", None),
            P(("seq", "fsdp"), None),
            P(("seq", "fsdp"), None),
            P(("seq", "fsdp"), None),
            P(("seq", "fsdp"), None),
            P(("seq", "fsdp"), None),
            P(("seq", "fsdp")),
            P(("seq", "fsdp")),
            P(("seq", "fsdp")),
            P(("seq", "fsdp")),
            P("seq", "fsdp", None),
            P("seq", "fsdp", None),
            P("seq", "fsdp", None),
        ),
        check_vma=False,
    )
```

time: 3800 us -> 1800 us (0.47)
  waiting for transfers between devices: 2890 us -> 787 us
  blocking collectives: 289 us -> 448 us
  local copies, waits for them, and re-layouts: 171 us -> 108 us
  matrix products: 273 us -> 226 us
  starting transfers between devices: 42.1 us -> 88.2 us
    reduce_scatter x7 -> x0, waiting for transfers between devices: 1970 us -> none  [the longest x1 365 us: body(): lax.psum_scatter(grad_key, ('seq', 'fsdp'), scatter_dimension=0, tiled=True)]
    all_gather x7 -> x6, waiting for transfers between devices: 663 us -> 66.3 us  [the longest x1 66.3 us: body(): mixed_all = lax.all_gather(mixed_low, 'fsdp', axis=0, tiled=False)]
    all_to_all x9 -> x18, waiting for transfers between devices: 242 us -> 583 us  [swap(): lax.all_to_all(values, axis_name, split_axis=dim, concat_axis=dim, tiled=...]
    all_gather x1 -> x5, blocking collectives: 115 us -> 335 us  [the longest x1 205 us: body(): small = lax.all_gather(small, AXES, axis=0, tiled=True)]
    unnamed x16 -> x10, waiting for transfers between devices: 3.96 us -> 137 us
    unnamed x2 -> x0, blocking collectives: 83.7 us -> none
    gather x4 -> x0, local copies, waits for them, and re-layouts: 56.4 us -> none  [the longest x1 16.8 us: body(): grad_back[safe_slot]]
    all_to_all x9 -> x18, starting transfers between devices: 37.2 us -> 82.9 us  [swap(): lax.all_to_all(values, axis_name, split_axis=dim, concat_axis=dim, tiled=...]
  transfers between devices with their start and end apart: 25 -> 27, of which waited for: 18 -> 14; matrix products, arithmetic and copies ran while one was open for 12% -> 22% of each run, Pallas kernels for 0% -> 0%
where the time goes in v1:
time: 1800 us; the launch traced here: 1790 us
  waiting for transfers between devices  787 us (44%)
  blocking collectives  448 us (25%)
  matrix products  226 us (13%)
  other arithmetic  111 us (6%)
  local copies, waits for them, and re-layouts  108 us (6%)
  starting transfers between devices  88.2 us (5%)
    all_to_all x18, waiting for transfers between devices, swap(): lax.all_to_all(values, axis_name, split_axis=dim, concat_axis=dim, tiled=...  583 us
    all_gather x1, blocking collectives, body(): small = lax.all_gather(small, AXES, axis=0, tiled=True)  205 us
    dot_general x34, matrix products, dot32(): return jnp.einsum(spec, left, right, preferred_element_type=jnp.float32)  199 us
    unnamed x10, waiting for transfers between devices  137 us
    all_gather x1, blocking collectives, body(): choice_all = lax.all_gather(chosen_ids, 'fsdp', axis=0, tiled=False)  97.6 us
    all_to_all x2, blocking collectives, swap(): lax.all_to_all(values, axis_name, split_axis=dim, concat_axis=dim, tiled=...  94.5 us
    all_to_all x18, starting transfers between devices, swap(): lax.all_to_all(values, axis_name, split_axis=dim, concat_axis=dim, tiled=...  82.9 us
    all_gather x1, waiting for transfers between devices, body(): mixed_all = lax.all_gather(mixed_low, 'fsdp', axis=0, tiled=False)  66.3 us
  transfers between devices with their start and end apart: 27, of which 14 were waited for; matrix products, arithmetic and copies ran while one was open for 22% of the time, Pallas kernels for 0%

profile of v1, /device:TPU:0, one launch (start us, length us, event | category | flops | bytes accessed | tf_op | source)
XLA Modules:
  0.0 1789.9 jit_solution(10543906054225686934)
XLA Ops:
  10.5 17.6 all_to_all.135
  35.4 205.4 %all-gather.5 = bf16[32,64,36]{1,2,0:T(8,128)(2,1)S(1)} all-gather(bf16[1,64,36]{1,2,0:T(8,128)(2,1)S(1)} %bitcast.320), channel_id=1, replica_groups=mesh['seq'=8,'fsdp'=4] {'seq','fsdp'}, dimensions={0}, use_global_device_ids=true | all-gather | bytes 152064 | tf_op jit(solution)/shard_map/all_gather | solution.py:197
  244.5 5.4 copy.241
  257.2 9.8 fusion.43
  271.6 8.5 all-gather.6
  301.8 26.4 %while.27 = (s32[]{:T(128)}, bf16[3,512,2,128]{3,2,1,0:T(2,128)(2,1)S(1)}, f32[3,2,512]{2,1,0:T(2,128)}, s32[3]{0:T(128)S(1)}, s32[1536]{0:T(1024)S(1)}, /*index...) while((s32[]{:T(128)}, ...), condition=%wide.region_10.11_spmd, body=%wide.region_7.10_spmd.sunk | while | flops 825097216 | bytes 24687292 | solution.py:117
  330.1 19.3 %all_to_all.136 = bf16[8,192,256]{2,1,0:T(8,128)(2,1)} all-to-all(bf16[8,192,256]{2,1,0:T(8,128)(2,1)} %all_to_all.87), channel_id=1, replica_groups=mesh['seq'=8,'fsdp'=4] {'seq'}, dimensions={0} | all-to-all | bytes 1572864 | tf_op jit(solution)/shard_map/all_to_all | solution.py:291
  354.3 97.6 %all_gather.53 = s32[4,192,8]{1,2,0:T(8,128)S(1)} all-gather(s32[1,192,8]{1,2,0:T(8,128)S(1)} %copy-done.49), channel_id=1, replica_groups=mesh['seq'=8,'fsdp'=4] {'fsdp'}, dimensions={0}, use_global_device_ids=true | all-gather | bytes 30720 | tf_op jit(solution)/shard_map/all_gather | solution.py:243
  463.9 5.6 multiply_reduce_fusion.5
  475.5 66.3 %all-gather.25.cloned.1.call-done = bf16[768,2048]{1,0:T(8,128)(2,1)} async-done(((bf16[192,2048]{1,0:T(8,128)(2,1)}), bf16[768,2048]{1,0:T(8,128)(2,1)}) %all-gather.25.cloned.1.call-update) | async-done | bytes 3145744 | tf_op jit(solution)/shard_map/all_gather | solution.py:298
  548.8 76.9 %all_to_all.137 = bf16[4,8,48,2048]{3,2,0,1:T(8,128)(2,1)} all-to-all(bf16[4,8,48,2048]{3,2,0,1:T(8,128)(2,1)} %copy.251), channel_id=1, replica_groups=mesh['seq'=8,'fsdp'=4] {'seq'}, dimensions={1} | all-to-all | bytes 12582912 | tf_op jit(solution)/shard_map/all_to_all | solution.py:93
  630.7 6.7 copy.258
  641.3 12.1 fusion.98
  653.4 10.5 fusion.99
  663.9 59.8 %all-to-all-done.5 = bf16[4,256,2048]{2,1,0:T(8,128)(2,1)} async-done(((bf16[4,256,2048]{2,1,0:T(8,128)(2,1)}), bf16[4,256,2048]{2,1,0:T(8,128)(2,1)}, u32[]{:S(2)}, u32[]{:S(2)}) %all-to-all-start.5) | async-done | bytes 4194336 | tf_op jit(solution)/shard_map/all_to_all | solution.py:93
  723.6 15.9 fusion.34
  743.6 13.4 all_gather.54
  758.7 5.9 fusion.33
  779.4 8.0 multiply_convert_fusion.1
  787.4 13.6 fusion.101
  801.1 11.1 add_convert_fusion
  815.4 5.2 all-to-all-start.10
  820.6 9.6 convolution_convert_fusion.1
  833.5 58.6 %all-to-all-done.10 = bf16[4,8,48,2048]{3,2,0,1:T(8,128)(2,1)} async-done(((bf16[4,8,48,2048]{3,2,0,1:T(8,128)(2,1)}), bf16[4,8,48,2048]{3,2,0,1:T(8,128)(2,1)}, u32[]{:S(2)}, u32[]{:S(2)}) %all-to-all-start.10) | async-done | bytes 6291488 | tf_op jit(solution)/shard_map/all_to_all | solution.py:93
  903.9 64.7 %all-to-all-done.6 = bf16[4,8,48,2048]{3,2,0,1:T(8,128)(2,1)} async-done(((bf16[4,8,48,2048]{3,2,0,1:T(8,128)(2,1)}), bf16[4,8,48,2048]{3,2,0,1:T(8,128)(2,1)}, u32[]{:S(2)}, u32[]{:S(2)}) %all-to-all-start.6) | async-done | bytes 6291488 | tf_op jit(solution)/shard_map/all_to_all | solution.py:93
  973.6 11.4 convolution_convert_fusion.2
  985.0 56.5 %all-to-all-done.11 = bf16[4,192,2048]{2,1,0:T(8,128)(2,1)} async-done(((bf16[4,192,2048]{2,1,0:T(8,128)(2,1)}), bf16[4,192,2048]{2,1,0:T(8,128)(2,1)}, u32[]{:S(2)}, u32[]{:S(2)}) %all-to-all-start.11) | async-done | bytes 3145760 | tf_op jit(solution)/shard_map/all_to_all | solution.py:93
  1052.9 6.6 convolution_convert_fusion.9
  1060.4 79.0 %all-to-all-done.21 = bf16[4,256,2048]{2,1,0:T(8,128)(2,1)} async-done(((bf16[4,256,2048]{2,1,0:T(8,128)(2,1)}), bf16[4,256,2048]{2,1,0:T(8,128)(2,1)}, u32[]{:S(2)}, u32[]{:S(2)}) %all-to-all-start.21) | async-done | bytes 4194336 | tf_op jit(solution)/shard_map/all_to_all | solution.py:93
  1144.3 11.6 convolution_convert_fusion.4
  1161.8 11.6 convolution_convert_fusion.3
  1173.6 81.4 %all-to-all-done.19 = bf16[4,512,1024]{2,1,0:T(8,128)(2,1)} async-done(((bf16[4,512,1024]{2,1,0:T(8,128)(2,1)}), bf16[4,512,1024]{2,1,0:T(8,128)(2,1)}, u32[]{:S(2)}, u32[]{:S(2)}) %all-to-all-start.19) | async-done | bytes 4194336 | tf_op jit(solution)/shard_map/all_to_all | solution.py:93
  1255.0 5.2 all-to-all-start.20
  1260.2 59.9 %while.28 = (s32[]{:T(128)}, f32[1536,2,128]{0,2,1:T(8,128)}, f32[1536,2,128]{0,2,1:T(8,128)}, f32[3,512,2,128]{3,1,0,2:T(8,128)}, s32[3]{0:T(128)S(1)}, /*index...) while((s32[]{:T(128)}, f32[1536,2,128]{0,2,1:T(8,128)}, ...), condition=%wide.region_29.30_spmd.clone, body=%wide.region_27.29_spmd.clone.sunk | while | flops 2030304256 | bytes 122454952 | solution.py:146
  1337.9 9.8 all-gather.7
  1352.1 9.2 convolution_convert_fusion.7
  1375.3 64.2 %all-to-all-done.16 = bf16[8,4,64,768]{3,2,0,1:T(8,128)(2,1)S(1)} async-done(((bf16[8,4,64,768]{3,2,0,1:T(8,128)(2,1)}), bf16[8,4,64,768]{3,2,0,1:T(8,128)(2,1)S(1)}, u32[]{:S(2)}, u32[]{:S(2)}) %all-to-all-start.16) | async-done | bytes 3145760 | tf_op jit(solution)/shard_map/all_to_all | solution.py:93
  1450.0 67.2 %all-to-all-done.7 = bf16[4,192,2048]{2,1,0:T(8,128)(2,1)S(1)} async-done(((bf16[4,192,2048]{2,1,0:T(8,128)(2,1)}), bf16[4,192,2048]{2,1,0:T(8,128)(2,1)S(1)}, u32[]{:S(2)}, u32[]{:S(2)}) %all-to-all-start.7) | async-done | bytes 3145760 | tf_op jit(solution)/shard_map/all_to_all | solution.py:93
  1521.5 9.2 convolution_convert_fusion
  1530.7 9.4 all-to-all-done.17
  1540.0 5.1 all-to-all-start.15
  1548.9 6.7 convert_element_type.237
  1555.5 6.6 convert_element_type.232
  1562.2 6.6 convert_element_type.234
  1580.4 37.9 %all-to-all-done.15 = bf16[8,192,2048]{2,1,0:T(8,128)(2,1)} async-done(((bf16[8,192,2048]{2,1,0:T(8,128)(2,1)}), bf16[8,192,2048]{2,1,0:T(8,128)(2,1)}, u32[]{:S(2)}, u32[]{:S(2)}) %all-to-all-start.15) | async-done | bytes 6291488 | tf_op jit(solution)/shard_map/all_to_all | solution.py:93
  1618.3 5.3 convert_reduce_fusion
  1623.6 5.6 convolution_convert_fusion.8
  1642.7 134.4 %reduce-scatter.7.cloned.1.call-done = f32[64,34]{1,0:T(8,128)} async-done(((f32[2048,34]{1,0:T(8,128)}), f32[64,34]{1,0:T(8,128)}) %reduce-scatter.7.cloned.1.call-update) | async-done | bytes 8720
  (415 shorter events, 321.5 us)
Async XLA Ops:
  7.2 237.3 %all-gather.23.cloned.1.call-start = ((), (), s32[]{:S(2)}) async-start(), calls=%async_computation.28 | async-start | bytes 3932160 | tf_op jit(solution)/shard_map/all_gather | solution.py:212
  28.2 224.3 %all-gather.21.cloned.1.call-start = ((), (), s32[]{:S(2)}) async-start(), calls=%async_computation.27 | async-start | bytes 7077888 | tf_op jit(solution)/shard_map/all_gather | solution.py:207
  28.9 426.9 %all-gather.17.cloned.1.call-start = ((), (), s32[]{:S(2)}) async-start(), calls=%async_computation.25 | async-start | bytes 3932160 | tf_op jit(solution)/shard_map/all_gather | solution.py:264
  29.7 211.5 %copy-start.64 = (s32[1,1536]{1,0:T(1,128)S(1)}, s32[1,1536]{1,0:T(1,128)}, u32[]{:S(2)}) copy-start(s32[1,1536]{1,0:T(1,128)} %param.35) | copy-start | bytes 18436
  29.7 211.6 %copy-start.69 = (s32[1,2]{1,0:T(1,128)S(1)}, s32[1,2]{1,0:T(1,128)}, u32[]{:S(2)}) copy-start(s32[1,2]{1,0:T(1,128)} %param.36) | copy-start | bytes 28
  29.7 300.3 %all-to-all-start.3 = ((bf16[4,512,1024]{2,1,0:T(8,128)(2,1)}), bf16[4,512,1024]{2,1,0:T(8,128)(2,1)}, u32[]{:S(2)}, u32[]{:S(2)}) async-start(bf16[4,512,1024]{2,1,0:T(8,128)(2,1)} %param.31), calls=%async_computation.3 | async-start | bytes 8388608 | tf_op jit(solution)/shard_map/all_to_all | solution.py:93
  34.8 429.2 %all-gather.15.cloned.1.call-start = ((), (), s32[]{:S(2)}) async-start(), calls=%async_computation.24 | async-start | bytes 8650752 | tf_op jit(solution)/shard_map/all_gather | solution.py:214
  241.1 15.7 copy-start.50
  241.1 810.2 %copy-start.43 = (f32[2048,1]{0,1:T(1,128)}, f32[2048,1]{0,1:T(1,128)S(1)}, u32[]{:S(2)}) copy-start(f32[2048,1]{0,1:T(1,128)S(1)} %get-tuple-element.398) | copy-start | bytes 24580
  241.2 39.0 %copy-start.55 = (f32[256,1]{0,1:T(1,128)}, f32[256,1]{0,1:T(1,128)S(1)}, u32[]{:S(2)}) copy-start(f32[256,1]{0,1:T(1,128)S(1)} %get-tuple-element.406) | copy-start | bytes 3076
  241.2 39.0 %copy-start.57 = (f32[256,1]{0,1:T(1,128)}, f32[256,1]{0,1:T(1,128)S(1)}, u32[]{:S(2)}) copy-start(f32[256,1]{0,1:T(1,128)S(1)} %get-tuple-element.407) | copy-start | bytes 3076
  244.5 52.8 %copy-start.21 = (f32[1536,64]{1,0:T(8,128)}, f32[1536,64]{1,0:T(8,128)S(1)}, u32[]{:S(2)}) copy-start(f32[1536,64]{1,0:T(8,128)S(1)} %get-tuple-element.404) | copy-start | bytes 1179652
  244.5 52.8 %copy-start.23 = (f32[1536,64]{1,0:T(8,128)}, f32[1536,64]{1,0:T(8,128)S(1)}, u32[]{:S(2)}) copy-start(f32[1536,64]{1,0:T(8,128)S(1)} %get-tuple-element.405) | copy-start | bytes 1179652
  256.8 10.2 copy-start.62
  328.2 21.1 %copy-start.2 = (bf16[1536,2,128]{2,0,1:T(8,128)(2,1)}, bf16[1536,2,128]{2,0,1:T(8,128)(2,1)S(1)}, u32[]{:S(2)}) copy-start(bf16[1536,2,128]{2,0,1:T(8,128)(2,1)S(1)} %get-tuple-element.627) | copy-start | bytes 2359300
  328.3 21.1 %copy-start.5 = (bf16[1536,2,128]{2,0,1:T(8,128)(2,1)}, bf16[1536,2,128]{2,0,1:T(8,128)(2,1)S(1)}, u32[]{:S(2)}) copy-start(bf16[1536,2,128]{2,0,1:T(8,128)(2,1)S(1)} %get-tuple-element.644) | copy-start | bytes 2359300
  328.3 21.1 %copy-start.25 = (bf16[3,512,2,128]{3,2,1,0:T(2,128)(2,1)}, bf16[3,512,2,128]{3,2,1,0:T(2,128)(2,1)S(1)}, u32[]{:S(2)}) copy-start(bf16[3,512,2,128]{3,2,1,0:T(2,128)(2,1)S(1)} %get-tuple-element.116) | copy-start | bytes 2359300
  328.3 21.1 %copy-start.36 = (s32[1536]{0:T(1024)}, s32[1536]{0:T(1024)S(1)}, u32[]{:S(2)}) copy-start(s32[1536]{0:T(1024)S(1)} %get-tuple-element.709) | copy-start | bytes 18436
  328.3 131.3 %copy-start.8 = (bf16[1536,2,128]{2,0,1:T(8,128)(2,1)}, bf16[1536,2,128]{2,0,1:T(8,128)(2,1)S(1)}, u32[]{:S(2)}) copy-start(bf16[1536,2,128]{2,0,1:T(8,128)(2,1)S(1)} %get-tuple-element.662) | copy-start | bytes 2359300
  349.4 120.2 %all-to-all-start.4 = ((bf16[4,512,1024]{2,1,0:T(8,128)(2,1)}), bf16[4,512,1024]{2,1,0:T(8,128)(2,1)}, u32[]{:S(2)}, u32[]{:S(2)}) async-start(bf16[4,512,1024]{2,1,0:T(8,128)(2,1)} %param.32), calls=%async_computation.4 | async-start | bytes 8388608 | tf_op jit(solution)/shard_map/all_to_all | solution.py:93
  455.8 444.6 %copy-start.18 = (pred[4,192,384]{2,1,0:T(32,128)(4,1)}, pred[4,192,384]{2,1,0:T(32,128)(4,1)S(1)}, u32[]{:S(2)}) copy-start(pred[4,192,384]{2,1,0:T(32,128)(4,1)S(1)} %bitcast_and_fusion) | copy-start | bytes 884740
  469.5 581.8 %copy-start.9 = (f32[192,2048]{1,0:T(8,128)}, f32[192,2048]{1,0:T(8,128)S(1)}, u32[]{:S(2)}) copy-start(f32[192,2048]{1,0:T(8,128)S(1)} %get-tuple-element.409) | copy-start | bytes 4718596
  469.5 581.7 %copy-start.53 = (f32[192]{0:T(256)}, f32[192]{0:T(256)S(1)}, u32[]{:S(2)}) copy-start(f32[192]{0:T(256)S(1)} %add_rsqrt_fusion.2) | copy-start | bytes 2308
  469.6 79.3 %all-to-all-start.9 = ((bf16[4,8,48,2048]{3,2,0,1:T(8,128)(2,1)}), bf16[4,8,48,2048]{3,2,0,1:T(8,128)(2,1)}, u32[]{:S(2)}, u32[]{:S(2)}) async-start(bf16[4,8,48,2048]{3,2,0,1:T(8,128)(2,1)} %copy.257), calls=%async_computation.9 | async-start | bytes 12582912 | tf_op jit(solution)/shard_map/all_to_all | solution.py:93
  474.3 67.5 %all-gather.25.cloned.1.call-start = ((), (), s32[]{:S(2)}) async-start(), calls=%async_computation.29 | async-start | bytes 3932160 | tf_op jit(solution)/shard_map/all_gather | solution.py:298
  625.7 98.0 %all-to-all-start.5 = ((bf16[4,256,2048]{2,1,0:T(8,128)(2,1)}), bf16[4,256,2048]{2,1,0:T(8,128)(2,1)}, u32[]{:S(2)}, u32[]{:S(2)}) async-start(bf16[4,256,2048]{2,1,0:T(8,128)(2,1)} %param.33), calls=%async_computation.5 | async-start | bytes 8388608 | tf_op jit(solution)/shard_map/all_to_all | solution.py:93
  641.3 12.1 copy-start.28
  740.3 16.9 all-to-all-start.12
  766.5 8.8 all-to-all-start.8
  775.3 40.1 %all-to-all-start.13 = ((f32[4,192,8]{1,2,0:T(8,128)}), f32[4,192,8]{1,2,0:T(8,128)S(1)}, u32[]{:S(2)}, u32[]{:S(2)}) async-start(f32[4,192,8]{1,2,0:T(8,128)} %copy.263), calls=%async_computation.13 | async-start | bytes 65536 | tf_op jit(solution)/shard_map/all_to_all | solution.py:93
  787.4 13.7 copy-start.35
  787.4 13.6 copy-start.34
  815.4 76.8 %all-to-all-start.10 = ((bf16[4,8,48,2048]{3,2,0,1:T(8,128)(2,1)}), bf16[4,8,48,2048]{3,2,0,1:T(8,128)(2,1)}, u32[]{:S(2)}, u32[]{:S(2)}) async-start(bf16[4,8,48,2048]{3,2,0,1:T(8,128)(2,1)} %copy.259), calls=%async_computation.10 | async-start | bytes 12582912 | tf_op jit(solution)/shard_map/all_to_all | solution.py:93
  892.2 76.3 %all-to-all-start.6 = ((bf16[4,8,48,2048]{3,2,0,1:T(8,128)(2,1)}), bf16[4,8,48,2048]{3,2,0,1:T(8,128)(2,1)}, u32[]{:S(2)}, u32[]{:S(2)}) async-start(bf16[4,8,48,2048]{3,2,0,1:T(8,128)(2,1)} %copy.253), calls=%async_computation.6 | async-start | bytes 12582912 | tf_op jit(solution)/shard_map/all_to_all | solution.py:93
  968.5 73.0 %all-to-all-start.11 = ((bf16[4,192,2048]{2,1,0:T(8,128)(2,1)}), bf16[4,192,2048]{2,1,0:T(8,128)(2,1)}, u32[]{:S(2)}, u32[]{:S(2)}) async-start(bf16[4,192,2048]{2,1,0:T(8,128)(2,1)} %convolution_convert_fusion.6), calls=%async_computation.11 | async-start | bytes 6291456 | tf_op jit(solution)/shard_map/all_to_all | solution.py:93
  1041.6 97.8 %all-to-all-start.21 = ((bf16[4,256,2048]{2,1,0:T(8,128)(2,1)}), bf16[4,256,2048]{2,1,0:T(8,128)(2,1)}, u32[]{:S(2)}, u32[]{:S(2)}) async-start(bf16[4,256,2048]{2,1,0:T(8,128)(2,1)} %bitcast.278), calls=%async_computation.21 | async-start | bytes 8388608 | tf_op jit(solution)/shard_map/all_to_all | solution.py:93
  1139.4 17.5 all-to-all-start.14
  1156.9 98.1 %all-to-all-start.19 = ((bf16[4,512,1024]{2,1,0:T(8,128)(2,1)}), bf16[4,512,1024]{2,1,0:T(8,128)(2,1)}, u32[]{:S(2)}, u32[]{:S(2)}) async-start(bf16[4,512,1024]{2,1,0:T(8,128)(2,1)} %bitcast.279), calls=%async_computation.19 | async-start | bytes 8388608 | tf_op jit(solution)/shard_map/all_to_all | solution.py:93
  1255.0 108.3 %all-to-all-start.20 = ((bf16[4,512,1024]{2,1,0:T(8,128)(2,1)}), bf16[4,512,1024]{2,1,0:T(8,128)(2,1)}, u32[]{:S(2)}, u32[]{:S(2)}) async-start(bf16[4,512,1024]{2,1,0:T(8,128)(2,1)} %bitcast.277), calls=%async_computation.20 | async-start | bytes 8388608 | tf_op jit(solution)/shard_map/all_to_all | solution.py:93
  1363.2 76.2 %all-to-all-start.16 = ((bf16[8,4,64,768]{3,2,0,1:T(8,128)(2,1)}), bf16[8,4,64,768]{3,2,0,1:T(8,128)(2,1)S(1)}, u32[]{:S(2)}, u32[]{:S(2)}) async-start(bf16[8,4,64,768]{3,2,0,1:T(8,128)(2,1)} %copy.272), calls=%async_computation.16 | async-start | bytes 6291456 | tf_op jit(solution)/shard_map/all_to_all | solution.py:93
  1441.1 76.1 %all-to-all-start.7 = ((bf16[4,192,2048]{2,1,0:T(8,128)(2,1)}), bf16[4,192,2048]{2,1,0:T(8,128)(2,1)S(1)}, u32[]{:S(2)}, u32[]{:S(2)}) async-start(bf16[4,192,2048]{2,1,0:T(8,128)(2,1)} %convolution_convert_fusion.5), calls=%async_computation.7 | async-start | bytes 6291456 | tf_op jit(solution)/shard_map/all_to_all | solution.py:93
  1444.8 125.7 %reduce-scatter.9.cloned.1.call-start = ((), (), s32[]{:S(2)}) async-start(), calls=%async_computation.31 | async-start | bytes 163840
  1445.8 177.8 %all-gather.19.cloned.1.call-start = ((), (), s32[]{:S(2)}) async-start(), calls=%async_computation.26 | async-start | bytes 7077888 | tf_op jit(solution)/shard_map/all_gather | solution.py:352
  1517.2 22.8 %all-to-all-start.17 = ((bf16[8,64,768]{2,1,0:T(8,128)(2,1)}), bf16[8,64,768]{2,1,0:T(8,128)(2,1)}, u32[]{:S(2)}, u32[]{:S(2)}) async-start(bf16[8,64,768]{2,1,0:T(8,128)(2,1)} %reduce_sum.328), calls=%async_computation.17 | async-start | bytes 1572864 | tf_op jit(solution)/shard_map/all_to_all | solution.py:93
  1540.0 78.3 %all-to-all-start.15 = ((bf16[8,192,2048]{2,1,0:T(8,128)(2,1)}), bf16[8,192,2048]{2,1,0:T(8,128)(2,1)}, u32[]{:S(2)}, u32[]{:S(2)}) async-start(bf16[8,192,2048]{2,1,0:T(8,128)(2,1)} %bitcast.272), calls=%async_computation.15 | async-start | bytes 12582912 | tf_op jit(solution)/shard_map/all_to_all | solution.py:93
  1580.4 43.2 %copy-start.26 = (bf16[3,512,2,128]{3,2,1,0:T(2,128)(2,1)S(1)}, bf16[3,512,2,128]{3,2,1,0:T(2,128)(2,1)}, u32[]{:S(2)}) copy-start(bf16[3,512,2,128]{3,2,1,0:T(2,128)(2,1)} %copy-done.25) | copy-start | bytes 2359300
  1629.2 151.4 %all-to-all-start.18 = ((bf16[4,64,2048]{2,1,0:T(8,128)(2,1)}), bf16[4,64,2048]{2,1,0:T(8,128)(2,1)}, u32[]{:S(2)}, u32[]{:S(2)}) async-start(bf16[4,64,2048]{2,1,0:T(8,128)(2,1)} %bitcast.57), calls=%async_computation.18 | async-start | bytes 2097152 | tf_op jit(solution)/shard_map/all_to_all | solution.py:93
  1633.7 143.5 %reduce-scatter.7.cloned.1.call-start = ((), (), s32[]{:S(2)}) async-start(), calls=%async_computation.30 | async-start | bytes 1081344
  (61 other events, 259.7 us)
Sparse Core Ops, SparseCore 0:
  28.3 131.9 all-gather.22
  162.2 45.7 all-gather.20
  209.6 64.3 all-gather.16
  276.7 82.9 all-gather.14
  476.4 65.3 all-gather.24
  1448.2 25.7 reduce-scatter.8
  1475.8 77.1 all-gather.18
  1638.5 138.6 reduce-scatter.6
